TPU v7x, 256 devices: a whole 4x4x8 slice. The times are simulated.
256 devices in a mesh: seq: 32 (over y, z), head: 8 (over x, core).
Axes of the slice: x: 4, y: 4, z: 8, core: 2. Of those that a mesh axis runs over, the one named last changes fastest.
Arguments:
- tokens: bfloat16 [12288, 4096], P('seq', 'head'), may hold values from -6 to 6
- norm_gain: float32 [4096], replicated, may hold values from 0.25 to 1.75
- w_in: bfloat16 [4096, 8, 2304], P('seq', 'head'), may hold values from -0.09375 to 0.09375
- w_dt: bfloat16 [4096, 128], P('seq', 'head'), may hold values from -0.09375 to 0.09375
- dt_bias: float32 [128], P('head'), may hold values from -3 to -1
- a_log: float32 [128], P('head'), may hold values from -11 to -1
- d_skip: float32 [128], P('head'), may hold values from 0.5 to 1.5
- conv_w: float32 [4, 8, 1280], P(None, 'head'), may hold values from -0.5 to 0.5
- conv_b: float32 [8, 1280], P('head'), may hold values from -0.5 to 0.5
- gate_gain: float32 [8, 1024], P('head'), may hold values from 0.25 to 1.75
- w_out: bfloat16 [8, 1024, 4096], P('head'), may hold values from -0.09375 to 0.09375
Outputs:
- mixed: bfloat16 [12288, 4096], P('seq', 'head')
All inputs are finite; a program needn't handle non-finite values.
Results may differ from a plain program's by a relative error of at most 0.018.
Values may be sent and summed in bfloat16 or wider, within the bound.
A program may use at most 128 MiB of HBM per device.

v0:
```python
from functools import partial
import jax
import jax.numpy as jnp
from jax import lax
from jax.sharding import Mesh
from jax.sharding import PartitionSpec as P

STRETCH = 128
SEQ = ("seq_0", "seq_1")
EPS = 1e-05
HIGHEST = lax.Precision.HIGHEST


def from_behind(shard, axis, by):
    count = lax.axis_size(axis)
    pairs = [(i, i + by) for i in range(count) if 0 <= i + by < count]
    return lax.ppermute(shard, axis, pairs)


def sent_together(arrays, axis, dim, along):
    both = jnp.concatenate(arrays, axis=along)
    result, at, gathered = (lax.all_gather(both, axis, axis=dim, tiled=True), 0, [])
    for a in arrays:
        gathered.append(lax.slice_in_dim(result, at, at + a.shape[along], axis=along))
        at += a.shape[along]
    return tuple(gathered)


def neutral_like(shard, identity):
    return jax.tree.map(
        lambda part, zero: jnp.zeros_like(part) + jnp.asarray(zero, part.dtype), shard, identity
    )


def entering(shard, axes, combine, identity):
    before = start = neutral_like(shard, identity)
    running = shard
    for axis in reversed(axes):
        count, index = (lax.axis_size(axis), lax.axis_index(axis))
        pieces = jax.tree.map(
            lambda part, kind: lax.all_gather(part.astype(kind), axis),
            running,
            (jnp.bfloat16, jnp.bfloat16),
        )
        inside, running = (start, start)
        for k in range(count):
            passed = k < index
            running = combine(
                running, jax.tree.map(lambda part, own: part[k].astype(own.dtype), pieces, shard)
            )
            inside = jax.tree.map(lambda new, old: jnp.where(passed, new, old), running, inside)
        before = combine(inside, before)
    return before


def normalize(values, gain):
    squares = jnp.mean(values * values, axis=-1, keepdims=True)
    return values * lax.rsqrt(squares + EPS) * gain


def state_block(inputs, step_size, log_decay, in_map, out_map, block_len):
    length = inputs.shape[0]
    stretch_count = length // block_len
    head_count = inputs.shape[1]
    head_size = inputs.shape[2]
    state_size = in_map.shape[1]
    shaped = (
        inputs.reshape(stretch_count, block_len, head_count, head_size),
        step_size.reshape(stretch_count, block_len, head_count),
        log_decay.reshape(stretch_count, block_len, head_count),
        in_map.reshape(stretch_count, block_len, state_size),
        out_map.reshape(stretch_count, block_len, state_size),
    )
    causal = jnp.arange(block_len)[:, None] >= jnp.arange(block_len)[None, :]

    def advance(state_now, pieces):
        stretch_in, stretch_step, stretch_log, stretch_b, stretch_c = pieces
        cumulative = jnp.cumsum(stretch_log, axis=0)
        gap_log = cumulative[:, None, :] - cumulative[None, :, :]
        decays = jnp.where(
            causal[:, :, None], jnp.exp(jnp.where(causal[:, :, None], gap_log, 0.0)), 0.0
        )
        scores = jnp.dot(stretch_c, stretch_b.T, preferred_element_type=jnp.float32)
        wide_c = stretch_c.astype(jnp.float32)
        wide_b = stretch_b.astype(jnp.float32)
        weights = scores[:, :, None] * decays * stretch_step[None, :, :]
        within = jnp.einsum("ijh,jhp->ihp", weights, stretch_in, precision=HIGHEST)
        across = jnp.exp(cumulative)[:, :, None] * jnp.einsum(
            "in,hpn->ihp", wide_c, state_now, precision=HIGHEST
        )
        to_end = jnp.exp(cumulative[-1][None, :] - cumulative) * stretch_step
        fresh_state = jnp.einsum("jh,jhp,jn->hpn", to_end, stretch_in, wide_b, precision=HIGHEST)
        state_next = jnp.exp(cumulative[-1])[:, None, None] * state_now + fresh_state
        return (state_next, within + across)

    start_state = jnp.zeros((head_count, head_size, state_size), jnp.float32)
    final, outputs = lax.scan(advance, start_state, shaped)
    return (outputs.reshape(length, head_count, head_size), final)


def link_states(earlier, later):
    return (earlier[0] + later[0], jnp.exp(later[0])[:, :, None, None] * earlier[1] + later[1])


def body(tokens, norm_gain, w_in, w_dt, dt_bias, a_log, d_skip, conv_w, conv_b, gate_gain, w_out):
    local_rows = tokens.shape[0]
    kernel_len = conv_w.shape[0]
    groups, group_width = gate_gain.shape
    head_count = dt_bias.shape[0]
    per_group = head_count // groups
    head_size = group_width // per_group
    state_size = (conv_b.shape[1] - group_width) // 2
    gathered = lax.all_gather(tokens, "head", axis=1, tiled=True)
    normed = normalize(gathered.astype(jnp.float32), norm_gain).astype(jnp.bfloat16)
    before = from_behind(normed[local_rows - kernel_len + 1 :], SEQ, 1)
    source = jnp.concatenate([before, normed], axis=0)
    span_rows = source.shape[0]
    flat_in = w_in.reshape(w_in.shape[0], groups * w_in.shape[2])
    pieces = sent_together((flat_in, w_dt), SEQ, 0, 1)
    proj_sum = jnp.dot(source, pieces[0], preferred_element_type=jnp.float32)
    step_sum = jnp.dot(source, pieces[1], preferred_element_type=jnp.float32)
    projected = proj_sum.astype(jnp.bfloat16).reshape(span_rows, groups, w_in.shape[2])
    step_size = jax.nn.softplus(step_sum[span_rows - local_rows :] + dt_bias[None, :])
    gate_raw = projected[span_rows - local_rows :, :, :group_width]
    extended = projected[:, :, group_width:]
    summed = conv_b[None, :, :]
    for offset in range(kernel_len):
        summed = summed + conv_w[offset][None, :, :] * extended[
            offset : offset + local_rows
        ].astype(jnp.float32)
    narrow = lax.optimization_barrier(jax.nn.silu(summed).astype(jnp.bfloat16))
    convolved = narrow.astype(jnp.float32)
    inputs = convolved[:, :, :group_width].reshape(local_rows, groups, per_group, head_size)
    in_map = narrow[:, :, group_width : group_width + state_size]
    out_map = narrow[:, :, group_width + state_size :]
    step_grouped = step_size.reshape(local_rows, groups, per_group)
    log_decay = -jnp.exp(a_log).reshape(groups, per_group)[None, :, :] * step_grouped
    run_block = jax.vmap(
        partial(state_block, block_len=STRETCH), in_axes=(1, 1, 1, 1, 1), out_axes=(1, 0)
    )
    local_out, ending = run_block(inputs, step_grouped, log_decay, in_map, out_map)
    totals = jnp.sum(log_decay, axis=0)
    identity = (jnp.zeros_like(totals), jnp.zeros_like(ending))
    prior_decay, incoming = entering((totals, ending), SEQ, link_states, identity)
    cumulative = jnp.exp(jnp.cumsum(log_decay, axis=0))
    carried = (
        jnp.einsum("tgn,ghpn->tghp", out_map.astype(jnp.float32), incoming, precision=HIGHEST)
        * cumulative[:, :, :, None]
    )
    outputs = local_out + carried + d_skip.reshape(groups, per_group)[None, :, :, None] * inputs
    gated = outputs.reshape(local_rows, groups, group_width) * jax.nn.silu(
        gate_raw.astype(jnp.float32)
    )
    normed_out = normalize(gated, gate_gain[None, :, :]).astype(jnp.bfloat16)
    flat_out = normed_out.reshape(local_rows, groups * group_width)
    terms = jnp.dot(
        flat_out,
        w_out.reshape(groups * group_width, w_out.shape[2]),
        preferred_element_type=jnp.float32,
    )
    return lax.psum_scatter(terms.astype(jnp.bfloat16), "head", scatter_dimension=1, tiled=True)


def solution(mesh):
    split = Mesh(mesh.devices.reshape(4, 8, mesh.shape["head"]), ("seq_0", "seq_1", "head"))
    in_specs = (
        P(SEQ, "head"),
        P(),
        P(SEQ, "head", None),
        P(SEQ, "head"),
        P("head"),
        P("head"),
        P("head"),
        P(None, "head", None),
        P("head", None),
        P("head", None),
        P("head", None, None),
    )
    out_specs = P(SEQ, "head")
    return jax.shard_map(body, mesh=split, in_specs=in_specs, out_specs=out_specs, check_vma=False)
```

profile of v0, /device:TPU:8, one launch (start us, length us, event | category | flops | bytes accessed | tf_op | source)
XLA Modules:
  0.0 413.0 jit_solution(1749421173129096668)
XLA Ops:
  6.5 0.7 all-gather.7.cloned.1.call-update
  7.3 0.8 copy.51
  8.1 2.0 pad_maximum_fusion
  10.2 32.1 %all-gather.7.cloned.1.call-done = bf16[384,4096]{1,0:T(8,128)(2,1)} async-done(((bf16[384,512]{1,0:T(8,128)(2,1)}), bf16[384,4096]{1,0:T(8,128)(2,1)}) %all-gather.7.cloned.1.call-update) | async-done | bytes 3145744 | tf_op jit(solution)/shard_map/all_gather | solution.py:113
  42.3 2.7 fusion.45
  45.1 1.1 fusion.47
  46.3 3.5 collective-permute-start
  49.9 4.3 %collective-permute-done = bf16[3,4096]{1,0:T(4,128)(2,1)S(1)} collective-permute-done((bf16[3,4096]{1,0:T(4,128)(2,1)S(1)}, bf16[3,4096]{1,0:T(4,128)(2,1)S(1)}, u32[]{:S(2)}, u32[]{:S(2)}) %collective-permute-start) | collective-permute-done | bytes 24608 | tf_op jit(solution)/shard_map/ppermute | solution.py:17
  54.2 145.0 %all-gather.9.cloned.1.call-done = bf16[4096,2320]{1,0:T(8,128)(2,1)} async-done(((bf16[128,2320]{1,0:T(8,128)(2,1)}), bf16[4096,2320]{1,0:T(8,128)(2,1)}) %all-gather.9.cloned.1.call-update) | async-done | bytes 19005456 | tf_op jit(solution)/shard_map/all_gather | solution.py:22
  199.2 13.4 %fusion.54 = bf16[387,1,2304]{2,0,1:T(8,128)(2,1)S(1)} fusion(bf16[4096,2320]{1,0:T(8,128)(2,1)} %all-gather.9.cloned.1.call-done, bf16[384,4096]{1,0:T(8,128)(2,1)} %copy-done.4, bf16[3,4096]{1,0:T(4,128)(2,1)S(1)} %collective-permute-done), kind=kOutput, calls=%fused_computation.61 | convolution fusion | flops 7311612928 | bytes 23827968 | tf_op jit(solution)/shard_map/dot_general | solution.py:120
  212.6 1.3 multiply_convert_fusion
  214.0 0.2 slice_convert_fusion
  214.1 1.3 copy-done.5
  215.5 2.3 fusion.162
  218.1 2.1 reshape.698
  220.2 3.2 copy.55
  223.4 59.6 %while.14 = (s32[]{:T(128)}, f32[1,16,64,128]{3,2,1,0:T(8,128)S(1)}, f32[3,1,128,16,64]{2,0,4,3,1:T(4,128)}, f32[3,1,128,16]{3,2,1,0:T(8,128)S(1)}, f32[3,1,128,...) while((s32[]{:T(128)}, ...), condition=%wide.region_3.4_spmd.clone.clone, body=%wide.region_1.3_spmd.clone.clone.sunk | while | flops 610682880 | bytes 5721559 | solution.py:97
  223.5 0.2 reduce_window_sum.44
  224.1 0.4 fusion.189
  224.5 3.3 fusion.191
  227.8 1.7 fusion.188
  229.4 13.8 %dynamic_update_slice.7 = f32[3,1,128,16,64]{2,0,4,3,1:T(4,128)} dynamic-update-slice(f32[3,1,128,16,64]{2,0,4,3,1:T(4,128)} %get-tuple-element.246, f32[1,1,128,16,64]{2,0,4,3,1:T(1,128)S(1)} %bitcast.242, s32[]{:T(128)S(6)} %copy.92, s32[]{:T(128)} %constant.25.clone.1..sunk, s32[]{:T(128)} %constant.25.clone.1..sunk, s32[]{:T(128)} %constant.25.clone.1..sunk, s32[]{:T(128)} %constant.25.clone.1..sunk) | dynamic-update-slice | bytes 1048580 | tf_op jit(solution)/shard_map/vmap()/while/body/jit(dynamic_update_index_in_dim)/dynamic_update_slice | solution.py:97
  243.3 0.2 reduce_window_sum.44
  244.0 0.4 fusion.189
  244.4 3.3 fusion.191
  247.7 1.7 fusion.188
  249.3 13.8 %dynamic_update_slice.7 = f32[3,1,128,16,64]{2,0,4,3,1:T(4,128)} dynamic-update-slice(f32[3,1,128,16,64]{2,0,4,3,1:T(4,128)} %get-tuple-element.246, f32[1,1,128,16,64]{2,0,4,3,1:T(1,128)S(1)} %bitcast.242, s32[]{:T(128)S(6)} %copy.92, s32[]{:T(128)} %constant.25.clone.1..sunk, s32[]{:T(128)} %constant.25.clone.1..sunk, s32[]{:T(128)} %constant.25.clone.1..sunk, s32[]{:T(128)} %constant.25.clone.1..sunk) | dynamic-update-slice | bytes 1048580 | tf_op jit(solution)/shard_map/vmap()/while/body/jit(dynamic_update_index_in_dim)/dynamic_update_slice | solution.py:97
  263.2 0.2 reduce_window_sum.44
  263.8 0.4 fusion.189
  264.3 3.3 fusion.191
  267.5 1.7 fusion.188
  269.2 13.8 %dynamic_update_slice.7 = f32[3,1,128,16,64]{2,0,4,3,1:T(4,128)} dynamic-update-slice(f32[3,1,128,16,64]{2,0,4,3,1:T(4,128)} %get-tuple-element.246, f32[1,1,128,16,64]{2,0,4,3,1:T(1,128)S(1)} %bitcast.242, s32[]{:T(128)S(6)} %copy.92, s32[]{:T(128)} %constant.25.clone.1..sunk, s32[]{:T(128)} %constant.25.clone.1..sunk, s32[]{:T(128)} %constant.25.clone.1..sunk, s32[]{:T(128)} %constant.25.clone.1..sunk) | dynamic-update-slice | bytes 1048580 | tf_op jit(solution)/shard_map/vmap()/while/body/jit(dynamic_update_index_in_dim)/dynamic_update_slice | solution.py:97
  283.0 0.7 convert_element_type.382
  283.9 0.6 dynamic-slice
  285.1 0.2 dynamic-update-slice
  285.4 15.7 %all-reduce = bf16[128]{0:T(256)(128)(2,1)S(1)} all-reduce(bf16[128]{0:T(256)(128)(2,1)S(1)} %dynamic-update-slice), channel_id=2, replica_groups=mesh['seq_0'=4,'seq_1'=8,'head'=8] {'seq_1'}, use_global_device_ids=true, to_apply=%add | all-reduce | flops 128 | bytes 512
  301.3 21.9 %all-gather.13.cloned.1.call-done = bf16[8,16,64,128]{3,2,1,0:T(8,128)(2,1)} async-done(((bf16[1,16,64,128]{3,2,1,0:T(8,128)(2,1)}), bf16[8,16,64,128]{3,2,1,0:T(8,128)(2,1)}) %all-gather.13.cloned.1.call-update) | async-done | bytes 2097168 | tf_op jit(solution)/shard_map/all_gather | solution.py:41
  323.1 2.8 fusion.106
  326.0 8.1 %all_gather.27 = bf16[4,1,16]{2,1,0:T(2,128)(2,1)S(1)} all-gather(bf16[1,1,16]{2,1,0:T(2,128)(2,1)S(1)} %get-tuple-element.156), channel_id=1, replica_groups=mesh['seq_0'=4,'seq_1'=8,'head'=8] {'seq_0'}, dimensions={0}, use_global_device_ids=true | all-gather | bytes 160 | tf_op jit(solution)/shard_map/all_gather | solution.py:41
  334.1 0.5 copy.62
  334.6 0.9 reduce-window.6
  335.8 2.8 transpose.64
  338.7 11.5 %all-gather.11.cloned.1.call-done = bf16[4,1,16,64,128]{4,3,2,1,0:T(8,128)(2,1)} async-done(((bf16[1,1,16,64,128]{4,3,2,1,0:T(8,128)(2,1)}), bf16[4,1,16,64,128]{4,3,2,1,0:T(8,128)(2,1)}) %all-gather.11.cloned.1.call-update) | async-done | bytes 1048592 | tf_op jit(solution)/shard_map/all_gather | solution.py:41
  350.2 4.7 %fusion.69 = f32[384,1,16,64]{0,3,2,1:T(8,128)} fusion(f32[384,1,16,64]{0,3,2,1:T(8,128)S(1)} %transpose.64, f32[384,1,16,64]{0,3,2,1:T(8,128)S(1)} %bitcast.245, f32[16]{0:T(128)S(1)} %copy-done.12, f32[384,16]{0,1:T(8,128)S(1)} %fusion.139, bf16[4,1,16,64,128]{4,3,2,1,0:T(8,128)(2,1)} %all-gather.11.cloned.1.call-done, f32[16]{0:T(128)S(1)} %get-tuple-element.173, ...), kind=kOutput, calls=%fused_computation.78 | convolution fusion | flops 611844096 | bytes 7988108 | tf_op jit(solution)/shard_map/tgn,ghpn->tghp/dot_general | solution.py:147
  354.9 2.0 copy.63
  356.9 0.7 multiply_reduce_fusion
  357.6 8.7 %fusion.48 = bf16[384,4096]{1,0:T(8,128)(2,1)} fusion(bf16[1,1024,4096]{2,1,0:T(8,128)(2,1)} %param.23, f32[1024]{0:T(1024)S(1)} %bitcast.251, f32[384]{0:T(512)S(1)} %add_rsqrt_fusion, f32[384,1,1024]{2,0,1:T(8,128)S(1)} %copy.63, bf16[387,1,2304]{2,0,1:T(8,128)(2,1)S(1)} %copy-done.2), kind=kOutput, calls=%fused_computation.59 | convolution fusion | flops 3226337280 | bytes 13899776 | tf_op jit(solution)/shard_map/dot_general | solution.py:156
  366.4 40.1 %reduce-scatter.2.cloned.1.call-done = bf16[384,512]{1,0:T(8,128)(2,1)} async-done(((bf16[384,4096]{1,0:T(8,128)(2,1)}), bf16[384,512]{1,0:T(8,128)(2,1)}) %reduce-scatter.2.cloned.1.call-update) | async-done | bytes 393232 | tf_op jit(solution)/shard_map/reduce_scatter | solution.py:161
  (90 shorter events, 2.8 us)
Async XLA Ops:
  6.5 3.6 copy-start.10
  6.5 35.8 %all-gather.7.cloned.1.call-start = ((), (), s32[]{:S(2)}) async-start(), calls=%async_computation.1 | async-start | bytes 3538944 | tf_op jit(solution)/shard_map/all_gather | solution.py:113
  7.3 191.9 %all-gather.9.cloned.1.call-start = ((), (), s32[]{:S(2)}) async-start(), calls=%async_computation.2 | async-start | bytes 20545536 | tf_op jit(solution)/shard_map/all_gather | solution.py:22
  10.1 34.9 %copy-start.7 = (f32[4096]{0:T(1024)S(1)}, f32[4096]{0:T(1024)}, u32[]{:S(2)}) copy-start(f32[4096]{0:T(1024)} %param.14) | copy-start | bytes 49156
  10.1 313.0 %all-gather.13.cloned.1.call-start = ((), (), s32[]{:S(2)}) async-start(), calls=%async_computation.5 | async-start | bytes 2359296 | tf_op jit(solution)/shard_map/all_gather | solution.py:41
  42.3 2.8 copy-start
  45.1 4.6 %copy-start.6 = (f32[4,1,1280]{2,1,0:T(1,128)S(1)}, f32[4,1,1280]{2,1,0:T(1,128)}, u32[]{:S(2)}) copy-start(f32[4,1,1280]{2,1,0:T(1,128)} %param.20) | copy-start | bytes 61444
  45.1 4.7 %copy-start.8 = (f32[1,1280]{1,0:T(1,128)S(1)}, f32[1,1280]{1,0:T(1,128)}, u32[]{:S(2)}) copy-start(f32[1,1280]{1,0:T(1,128)} %param.21) | copy-start | bytes 15364
  46.2 3.5 copy-start.4
  46.3 7.9 %collective-permute-start = (bf16[3,4096]{1,0:T(4,128)(2,1)S(1)}, bf16[3,4096]{1,0:T(4,128)(2,1)S(1)}, u32[]{:S(2)}, u32[]{:S(2)}) collective-permute-start(bf16[3,4096]{1,0:T(4,128)(2,1)S(1)} %slice.201), channel_id=1, source_target_pairs={{0,8},{8,16},{16,24},{24,32},{32,40},{40,48},{48,56},{56,64},{64,7... | collective-permute-start | bytes 73736 | tf_op jit(solution)/shard_map/ppermute | solution.py:17
  212.6 1.3 copy-start.1
  212.6 2.9 copy-start.5
  213.9 3.9 copy-start.3
  213.9 1.5 copy-start.11
  223.4 60.5 %copy-start.13 = (u32[256]{0:T(256)S(1)}, u32[256]{0:T(256)}, u32[]{:S(2)}) copy-start(u32[256]{0:T(256)} %constant.77) | copy-start | bytes 3076
  283.8 66.4 %all-gather.11.cloned.1.call-start = ((), (), s32[]{:S(2)}) async-start(), calls=%async_computation.3 | async-start | bytes 1310720 | tf_op jit(solution)/shard_map/all_gather | solution.py:41
  325.9 80.6 %reduce-scatter.2.cloned.1.call-start = ((), (), s32[]{:S(2)}) async-start(), calls=%async_computation.4 | async-start | bytes 3538944 | tf_op jit(solution)/shard_map/reduce_scatter | solution.py:161
  335.4 14.7 %copy-start.12 = (f32[16]{0:T(128)S(1)}, f32[16]{0:T(128)}, u32[]{:S(2)}) copy-start(f32[16]{0:T(128)} %param.19) | copy-start | bytes 196
  354.9 2.0 copy-start.2
  356.9 0.7 copy-start.9
Sparse Core Ops, SparseCore 0:
  9.2 33.0 all-gather.6
  44.9 154.2 all-gather.8
  283.9 39.1 all-gather.12
  326.1 24.0 all-gather.10
  366.5 39.9 reduce-scatter.1
where the time goes:
time: 415 us; the launch traced here: 413 us
  waiting for transfers between devices  256 us (62%)
  local copies, waits for them, and re-layouts  56.8 us (14%)
  matrix products  45.5 us (11%)
  blocking collectives  23.8 us (6%)
  between operations  14.1 us (3%)
  other arithmetic  13.3 us (3%)
    all_gather x1, waiting for transfers between devices, sent_together(): lax.all_gather(both, axis, axis=dim, tiled=True)  145 us
    dynamic_update_slice x3, local copies, waits for them, and re-layouts, state_block(): final, outputs = lax.scan(advance, start_state, shaped)  41.5 us
    reduce_scatter x1, waiting for transfers between devices, body(): lax.psum_scatter(terms.astype(jnp.bfloat16), 'head', scatter_dimension=1,...  40.1 us
    all_gather x2, waiting for transfers between devices, entering(): lax.all_gather(part.astype(kind), axis)  33.4 us
    all_gather x1, waiting for transfers between devices, body(): gathered = lax.all_gather(tokens, 'head', axis=1, tiled=True)  32.1 us
    unnamed x1, blocking collectives  15.7 us
    dot_general x1, matrix products, body(): proj_sum = jnp.dot(source, pieces[0], preferred_element_type=jnp.float32)  13.4 us
    dot_general x3, matrix products, advance(): within = jnp.einsum('ijh,jhp->ihp', weights, stretch_in, precision=HIGHEST)  9.81 us
  transfers between devices with their start and end apart: 6, of which 6 were waited for; matrix products, arithmetic and copies ran while one was open for 3% of the time, Pallas kernels for 0%

commit v1 on v0

--- a/solution.py
+++ b/solution.py
@@ -110,7 +110,24 @@
     per_group = head_count // groups
     head_size = group_width // per_group
     state_size = (conv_b.shape[1] - group_width) // 2
-    gathered = lax.all_gather(tokens, "head", axis=1, tiled=True)
+    size, index_2, rows = (lax.axis_size("head"), lax.axis_index("head"), tokens.shape[1])
+    right = [(i_2, (i_2 + 1) % size) for i_2 in range(size)]
+    left = [(i_2, (i_2 - 1) % size) for i_2 in range(size)]
+    out = jnp.zeros((*tokens.shape[:1], size * rows, *tokens.shape[1 + 1 :]), tokens.dtype)
+    out = lax.dynamic_update_slice_in_dim(out, tokens, index_2 * rows, axis=1)
+    from_left = from_right = tokens
+    half = size // 2
+    for step in range(1, half + 1):
+        from_left = lax.ppermute(from_left, "head", right)
+        out = lax.dynamic_update_slice_in_dim(
+            out, from_left, (index_2 - step) % size * rows, axis=1
+        )
+        if step < size - half:
+            from_right = lax.ppermute(from_right, "head", left)
+            out = lax.dynamic_update_slice_in_dim(
+                out, from_right, (index_2 + step) % size * rows, axis=1
+            )
+    gathered = out
     normed = normalize(gathered.astype(jnp.float32), norm_gain).astype(jnp.bfloat16)
     before = from_behind(normed[local_rows - kernel_len + 1 :], SEQ, 1)
     source = jnp.concatenate([before, normed], axis=0)

time: 415 us -> 389 us (0.937)
  waiting for transfers between devices: 256 us -> 213 us
  starting transfers between devices: 3.63 us -> 13 us
  local copies, waits for them, and re-layouts: 56.8 us -> 62.8 us
    all_gather x1, waiting for transfers between devices: 145 us -> 110 us  [sent_together(): lax.all_gather(both, axis, axis=dim, tiled=True)]
    all_gather x1 -> x0, waiting for transfers between devices: 32.1 us -> none  [body(): gathered = lax.all_gather(tokens, 'head', axis=1, tiled=True)]
    ppermute x0 -> x7, waiting for transfers between devices: none -> 23.6 us  [the longest x4 22.7 us: body(): from_left = lax.ppermute(from_left, 'head', right)]
    ppermute x0 -> x7, starting transfers between devices: none -> 8.88 us  [the longest x3 8.85 us: body(): from_right = lax.ppermute(from_right, 'head', left)]
    unnamed x35 -> x33, local copies, waits for them, and re-layouts: 6.62 us -> 9.58 us
  transfers between devices with their start and end apart: 6 -> 12, of which waited for: 6 -> 10; matrix products, arithmetic and copies ran while one was open for 3% -> 2% of each run, Pallas kernels for 0% -> 0%
where the time goes in v1:
time: 389 us; the launch traced here: 387 us
  waiting for transfers between devices  213 us (55%)
  local copies, waits for them, and re-layouts  62.8 us (16%)
  matrix products  45.7 us (12%)
  blocking collectives  23.9 us (6%)
  other arithmetic  14.5 us (4%)
  between operations  14.2 us (4%)
  starting transfers between devices  13 us (3%)
    all_gather x1, waiting for transfers between devices, sent_together(): lax.all_gather(both, axis, axis=dim, tiled=True)  110 us
    dynamic_update_slice x3, local copies, waits for them, and re-layouts, state_block(): final, outputs = lax.scan(advance, start_state, shaped)  41.5 us
    reduce_scatter x1, waiting for transfers between devices, body(): lax.psum_scatter(terms.astype(jnp.bfloat16), 'head', scatter_dimension=1,...  40.1 us
    all_gather x2, waiting for transfers between devices, entering(): lax.all_gather(part.astype(kind), axis)  33.4 us
    ppermute x4, waiting for transfers between devices, body(): from_left = lax.ppermute(from_left, 'head', right)  22.7 us
    unnamed x1, blocking collectives  15.7 us
    dot_general x1, matrix products, body(): proj_sum = jnp.dot(source, pieces[0], preferred_element_type=jnp.float32)  13.4 us
    dot_general x3, matrix products, advance(): within = jnp.einsum('ijh,jhp->ihp', weights, stretch_in, precision=HIGHEST)  9.79 us
  transfers between devices with their start and end apart: 12, of which 10 were waited for; matrix products, arithmetic and copies ran while one was open for 2% of the time, Pallas kernels for 0%

profile of v1, /device:TPU:8, one launch (start us, length us, event | category | flops | bytes accessed | tf_op | source)
XLA Modules:
  0.0 387.4 jit_solution(759592880242687121)
XLA Ops:
  7.3 2.0 pad_maximum_fusion
  9.4 2.9 collective-permute-start.1
  12.4 5.7 %collective-permute-done = bf16[384,512]{1,0:T(8,128)(2,1)S(1)} collective-permute-done((bf16[384,512]{1,0:T(8,128)(2,1)}, bf16[384,512]{1,0:T(8,128)(2,1)S(1)}, u32[]{:S(2)}, u32[]{:S(2)}) %collective-permute-start) | collective-permute-done | bytes 393248 | tf_op jit(solution)/shard_map/ppermute | solution.py:121
  18.0 3.0 collective-permute-start.3
  21.0 5.5 %collective-permute-done.2 = bf16[384,512]{1,0:T(8,128)(2,1)S(1)} collective-permute-done((bf16[384,512]{1,0:T(8,128)(2,1)S(1)}, bf16[384,512]{1,0:T(8,128)(2,1)S(1)}, u32[]{:S(2)}, u32[]{:S(2)}) %collective-permute-start.2) | collective-permute-done | bytes 393248 | tf_op jit(solution)/shard_map/ppermute | solution.py:121
  27.6 3.0 collective-permute-start.5
  30.6 4.2 %collective-permute-done.4 = bf16[384,512]{1,0:T(8,128)(2,1)S(1)} collective-permute-done((bf16[384,512]{1,0:T(8,128)(2,1)S(1)}, bf16[384,512]{1,0:T(8,128)(2,1)S(1)}, u32[]{:S(2)}, u32[]{:S(2)}) %collective-permute-start.4) | collective-permute-done | bytes 393248 | tf_op jit(solution)/shard_map/ppermute | solution.py:121
  35.0 0.8 collective-permute-done.5
  35.9 7.3 %collective-permute-done.6 = bf16[384,512]{1,0:T(8,128)(2,1)S(1)} collective-permute-done((bf16[384,512]{1,0:T(8,128)(2,1)S(1)}, bf16[384,512]{1,0:T(8,128)(2,1)S(1)}, u32[]{:S(2)}, u32[]{:S(2)}) %collective-permute-start.6) | collective-permute-done | bytes 393248 | tf_op jit(solution)/shard_map/ppermute | solution.py:121
  44.1 1.1 fusion.47
  45.2 1.7 copy-done.3
  46.9 4.0 %collective-permute-start.7 = (bf16[3,4096]{1,0:T(4,128)(2,1)S(1)}, bf16[3,4096]{1,0:T(4,128)(2,1)S(1)}, u32[]{:S(2)}, u32[]{:S(2)}) collective-permute-start(bf16[3,4096]{1,0:T(4,128)(2,1)S(1)} %slice.201), channel_id=1, source_target_pairs={{0,8},{8,16},{16,24},{24,32},{32,40},{40,48},{48,56},{56,64},{64,7... | collective-permute-start | bytes 73736 | tf_op jit(solution)/shard_map/ppermute | solution.py:17
  51.0 5.6 %collective-permute-done.7 = bf16[3,4096]{1,0:T(4,128)(2,1)S(1)} collective-permute-done((bf16[3,4096]{1,0:T(4,128)(2,1)S(1)}, bf16[3,4096]{1,0:T(4,128)(2,1)S(1)}, u32[]{:S(2)}, u32[]{:S(2)}) %collective-permute-start.7) | collective-permute-done | bytes 24608 | tf_op jit(solution)/shard_map/ppermute | solution.py:17
  56.7 110.5 %all-gather.6.cloned.1.call-done = bf16[4096,2320]{1,0:T(8,128)(2,1)} async-done(((bf16[128,2320]{1,0:T(8,128)(2,1)}), bf16[4096,2320]{1,0:T(8,128)(2,1)}) %all-gather.6.cloned.1.call-update) | async-done | bytes 19005456 | tf_op jit(solution)/shard_map/all_gather | solution.py:22
  167.1 13.4 %fusion.54 = bf16[387,1,2304]{2,0,1:T(8,128)(2,1)S(1)} fusion(bf16[4096,2320]{1,0:T(8,128)(2,1)} %all-gather.6.cloned.1.call-done, bf16[384,4096]{1,0:T(8,128)(2,1)} %copy-done.3, bf16[3,4096]{1,0:T(4,128)(2,1)S(1)} %collective-permute-done.7), kind=kOutput, calls=%fused_computation.61 | convolution fusion | flops 7311612928 | bytes 23827968 | tf_op jit(solution)/shard_map/dot_general | solution.py:137
  180.5 1.3 multiply_convert_fusion
  182.1 1.3 copy-done.4
  183.4 2.3 fusion.162
  185.7 0.8 copy.64
  187.4 2.1 reshape.698
  189.4 3.2 copy.55
  192.7 64.6 %while.14 = (s32[]{:T(128)}, f32[1,16,64,128]{3,2,1,0:T(8,128)S(1)}, f32[3,1,128,16,64]{2,0,4,3,1:T(4,128)}, f32[3,1,128,16]{3,2,1,0:T(8,128)}, f32[3,1,128,16]{...) while((s32[]{:T(128)}, ...), condition=%wide.region_3.4_spmd.clone.clone, body=%wide.region_1.3_spmd.clone.clone.sunk | while | flops 610682880 | bytes 5721559 | solution.py:97
  192.7 0.9 dynamic-slice_bitcast_fusion.4
  193.7 0.9 exponential_multiply_fusion.3
  195.1 1.7 fusion.188
  197.1 3.3 fusion.191
  200.4 13.8 %dynamic_update_slice.47 = f32[3,1,128,16,64]{2,0,4,3,1:T(4,128)} dynamic-update-slice(f32[3,1,128,16,64]{2,0,4,3,1:T(4,128)} %get-tuple-element.246, f32[1,1,128,16,64]{2,0,4,3,1:T(1,128)S(1)} %bitcast.242, s32[]{:T(128)S(6)} %copy.100, s32[]{:T(128)} %constant.97.clone.1..sunk, s32[]{:T(128)} %constant.97.clone.1..sunk, s32[]{:T(128)} %constant.97.clone.1..sunk, s32[]{:T(128)} %constant.97.clone.1..sunk) | dynamic-update-slice | bytes 1048580 | tf_op jit(solution)/shard_map/vmap()/while/body/jit(dynamic_update_index_in_dim)/dynamic_update_slice | solution.py:97
  214.2 0.8 dynamic-slice_bitcast_fusion.4
  215.2 0.9 exponential_multiply_fusion.3
  216.6 1.7 fusion.188
  218.6 3.3 fusion.191
  221.9 13.8 %dynamic_update_slice.47 = f32[3,1,128,16,64]{2,0,4,3,1:T(4,128)} dynamic-update-slice(f32[3,1,128,16,64]{2,0,4,3,1:T(4,128)} %get-tuple-element.246, f32[1,1,128,16,64]{2,0,4,3,1:T(1,128)S(1)} %bitcast.242, s32[]{:T(128)S(6)} %copy.100, s32[]{:T(128)} %constant.97.clone.1..sunk, s32[]{:T(128)} %constant.97.clone.1..sunk, s32[]{:T(128)} %constant.97.clone.1..sunk, s32[]{:T(128)} %constant.97.clone.1..sunk) | dynamic-update-slice | bytes 1048580 | tf_op jit(solution)/shard_map/vmap()/while/body/jit(dynamic_update_index_in_dim)/dynamic_update_slice | solution.py:97
  235.7 0.8 dynamic-slice_bitcast_fusion.4
  236.8 0.9 exponential_multiply_fusion.3
  238.2 1.7 fusion.188
  240.2 3.3 fusion.191
  243.4 13.8 %dynamic_update_slice.47 = f32[3,1,128,16,64]{2,0,4,3,1:T(4,128)} dynamic-update-slice(f32[3,1,128,16,64]{2,0,4,3,1:T(4,128)} %get-tuple-element.246, f32[1,1,128,16,64]{2,0,4,3,1:T(1,128)S(1)} %bitcast.242, s32[]{:T(128)S(6)} %copy.100, s32[]{:T(128)} %constant.97.clone.1..sunk, s32[]{:T(128)} %constant.97.clone.1..sunk, s32[]{:T(128)} %constant.97.clone.1..sunk, s32[]{:T(128)} %constant.97.clone.1..sunk) | dynamic-update-slice | bytes 1048580 | tf_op jit(solution)/shard_map/vmap()/while/body/jit(dynamic_update_index_in_dim)/dynamic_update_slice | solution.py:97
  259.6 15.7 %all-reduce = bf16[128]{0:T(256)(128)(2,1)S(1)} all-reduce(bf16[128]{0:T(256)(128)(2,1)S(1)} %dynamic-update-slice), channel_id=2, replica_groups=mesh['seq_0'=4,'seq_1'=8,'head'=8] {'seq_1'}, use_global_device_ids=true, to_apply=%add | all-reduce | flops 128 | bytes 512
  275.5 21.9 %all-gather.10.cloned.1.call-done = bf16[8,16,64,128]{3,2,1,0:T(8,128)(2,1)} async-done(((bf16[1,16,64,128]{3,2,1,0:T(8,128)(2,1)}), bf16[8,16,64,128]{3,2,1,0:T(8,128)(2,1)}) %all-gather.10.cloned.1.call-update) | async-done | bytes 2097168 | tf_op jit(solution)/shard_map/all_gather | solution.py:41
  297.4 2.8 fusion.106
  300.2 8.1 %all_gather.23 = bf16[4,1,16]{2,1,0:T(2,128)(2,1)S(1)} all-gather(bf16[1,1,16]{2,1,0:T(2,128)(2,1)S(1)} %get-tuple-element.156), channel_id=1, replica_groups=mesh['seq_0'=4,'seq_1'=8,'head'=8] {'seq_0'}, dimensions={0}, use_global_device_ids=true | all-gather | bytes 160 | tf_op jit(solution)/shard_map/all_gather | solution.py:41
  308.9 2.8 transpose.71
  311.7 0.9 reduce-window.6
  312.9 11.6 %all-gather.8.cloned.1.call-done = bf16[4,1,16,64,128]{4,3,2,1,0:T(8,128)(2,1)} async-done(((bf16[1,1,16,64,128]{4,3,2,1,0:T(8,128)(2,1)}), bf16[4,1,16,64,128]{4,3,2,1,0:T(8,128)(2,1)}) %all-gather.8.cloned.1.call-update) | async-done | bytes 1048592 | tf_op jit(solution)/shard_map/all_gather | solution.py:41
  324.5 4.7 %fusion.69 = f32[384,1,16,64]{0,3,2,1:T(8,128)} fusion(f32[384,1,16,64]{0,3,2,1:T(8,128)S(1)} %transpose.71, f32[384,1,16,64]{0,3,2,1:T(8,128)S(1)} %bitcast.245, f32[16]{0:T(128)S(1)} %copy-done.11, f32[384,16]{0,1:T(8,128)S(1)} %fusion.139, bf16[4,1,16,64,128]{4,3,2,1,0:T(8,128)(2,1)} %all-gather.8.cloned.1.call-done, f32[16]{0:T(128)S(1)} %get-tuple-element.173, ...), kind=kOutput, calls=%fused_computation.78 | convolution fusion | flops 611844096 | bytes 7988108 | tf_op jit(solution)/shard_map/tgn,ghpn->tghp/dot_general | solution.py:164
  329.2 2.0 copy.63
  331.9 8.8 %fusion.48 = bf16[384,4096]{1,0:T(8,128)(2,1)} fusion(bf16[1,1024,4096]{2,1,0:T(8,128)(2,1)} %param.23, f32[1024]{0:T(1024)S(1)} %bitcast.249, f32[384]{0:T(512)S(1)} %add_rsqrt_fusion, f32[384,1,1024]{2,0,1:T(8,128)S(1)} %copy.63, bf16[387,1,2304]{2,0,1:T(8,128)(2,1)S(1)} %copy-done.1), kind=kOutput, calls=%fused_computation.59 | convolution fusion | flops 3226337280 | bytes 13899776 | tf_op jit(solution)/shard_map/dot_general | solution.py:173
  340.7 40.1 %reduce-scatter.2.cloned.1.call-done = bf16[384,512]{1,0:T(8,128)(2,1)} async-done(((bf16[384,4096]{1,0:T(8,128)(2,1)}), bf16[384,512]{1,0:T(8,128)(2,1)}) %reduce-scatter.2.cloned.1.call-update) | async-done | bytes 393232 | tf_op jit(solution)/shard_map/reduce_scatter | solution.py:178
  (108 shorter events, 10.5 us)
Async XLA Ops:
  6.5 160.6 %all-gather.6.cloned.1.call-start = ((), (), s32[]{:S(2)}) async-start(), calls=%async_computation.1 | async-start | bytes 20545536 | tf_op jit(solution)/shard_map/all_gather | solution.py:22
  9.3 18.2 %copy-start.5 = (bf16[384,512]{1,0:T(8,128)(2,1)S(1)}, bf16[384,512]{1,0:T(8,128)(2,1)}, u32[]{:S(2)}) copy-start(bf16[384,512]{1,0:T(8,128)(2,1)} %param.13) | copy-start | bytes 1179652
  9.4 288.0 %all-gather.10.cloned.1.call-start = ((), (), s32[]{:S(2)}) async-start(), calls=%async_computation.4 | async-start | bytes 2359296 | tf_op jit(solution)/shard_map/all_gather | solution.py:41
  9.4 8.6 %collective-permute-start = (bf16[384,512]{1,0:T(8,128)(2,1)}, bf16[384,512]{1,0:T(8,128)(2,1)S(1)}, u32[]{:S(2)}, u32[]{:S(2)}) collective-permute-start(bf16[384,512]{1,0:T(8,128)(2,1)} %param.13), channel_id=1, source_target_pairs={{0,1},{1,2},{2,3},{3,4},{4,5},{5,6},{6,7},{7,0},{8,9},{9,10},{10,1... | collective-permute-start | bytes 1179656 | tf_op jit(solution)/shard_map/ppermute | solution.py:121
  9.4 8.6 %collective-permute-start.1 = (bf16[384,512]{1,0:T(8,128)(2,1)}, bf16[384,512]{1,0:T(8,128)(2,1)S(1)}, u32[]{:S(2)}, u32[]{:S(2)}) collective-permute-start(bf16[384,512]{1,0:T(8,128)(2,1)} %param.13), channel_id=1, source_target_pairs={{0,7},{1,0},{2,1},{3,2},{4,3},{5,4},{6,5},{7,6},{8,15},{9,8},{10,9... | collective-permute-start | bytes 1179656 | tf_op jit(solution)/shard_map/ppermute | solution.py:126
  18.0 8.4 %collective-permute-start.2 = (bf16[384,512]{1,0:T(8,128)(2,1)S(1)}, bf16[384,512]{1,0:T(8,128)(2,1)S(1)}, u32[]{:S(2)}, u32[]{:S(2)}) collective-permute-start(bf16[384,512]{1,0:T(8,128)(2,1)S(1)} %collective-permute-done), channel_id=1, source_target_pairs={{0,1},{1,2},{2,3},{3,4},{4,5},{5,6},{6,7},{7,0},{8,9},{9,10},{10,1... | collective-permute-start | bytes 1179656 | tf_op jit(solution)/shard_map/ppermute | solution.py:121
  18.0 9.6 %collective-permute-start.3 = (bf16[384,512]{1,0:T(8,128)(2,1)S(1)}, bf16[384,512]{1,0:T(8,128)(2,1)S(1)}, u32[]{:S(2)}, u32[]{:S(2)}) collective-permute-start(bf16[384,512]{1,0:T(8,128)(2,1)S(1)} %collective-permute-done.1), channel_id=1, source_target_pairs={{0,7},{1,0},{2,1},{3,2},{4,3},{5,4},{6,5},{7,6},{8,15},{9,8},{10,9... | collective-permute-start | bytes 1179656 | tf_op jit(solution)/shard_map/ppermute | solution.py:126
  26.5 8.4 %collective-permute-start.4 = (bf16[384,512]{1,0:T(8,128)(2,1)S(1)}, bf16[384,512]{1,0:T(8,128)(2,1)S(1)}, u32[]{:S(2)}, u32[]{:S(2)}) collective-permute-start(bf16[384,512]{1,0:T(8,128)(2,1)S(1)} %collective-permute-done.2), channel_id=1, source_target_pairs={{0,1},{1,2},{2,3},{3,4},{4,5},{5,6},{6,7},{7,0},{8,9},{9,10},{10,1... | collective-permute-start | bytes 1179656 | tf_op jit(solution)/shard_map/ppermute | solution.py:121
  27.6 8.3 %collective-permute-start.5 = (bf16[384,512]{1,0:T(8,128)(2,1)S(1)}, bf16[384,512]{1,0:T(8,128)(2,1)S(1)}, u32[]{:S(2)}, u32[]{:S(2)}) collective-permute-start(bf16[384,512]{1,0:T(8,128)(2,1)S(1)} %collective-permute-done.3), channel_id=1, source_target_pairs={{0,7},{1,0},{2,1},{3,2},{4,3},{5,4},{6,5},{7,6},{8,15},{9,8},{10,9... | collective-permute-start | bytes 1179656 | tf_op jit(solution)/shard_map/ppermute | solution.py:126
  34.9 8.4 %collective-permute-start.6 = (bf16[384,512]{1,0:T(8,128)(2,1)S(1)}, bf16[384,512]{1,0:T(8,128)(2,1)S(1)}, u32[]{:S(2)}, u32[]{:S(2)}) collective-permute-start(bf16[384,512]{1,0:T(8,128)(2,1)S(1)} %collective-permute-done.4), channel_id=1, source_target_pairs={{0,1},{1,2},{2,3},{3,4},{4,5},{5,6},{6,7},{7,0},{8,9},{9,10},{10,1... | collective-permute-start | bytes 1179656 | tf_op jit(solution)/shard_map/ppermute | solution.py:121
  35.9 8.1 %copy-start.7 = (f32[4096]{0:T(1024)S(1)}, f32[4096]{0:T(1024)}, u32[]{:S(2)}) copy-start(f32[4096]{0:T(1024)} %param.14) | copy-start | bytes 49156
  44.0 6.9 %copy-start.6 = (f32[4,1,1280]{2,1,0:T(1,128)S(1)}, f32[4,1,1280]{2,1,0:T(1,128)}, u32[]{:S(2)}) copy-start(f32[4,1,1280]{2,1,0:T(1,128)} %param.20) | copy-start | bytes 61444
  44.1 6.9 %copy-start.8 = (f32[1,1280]{1,0:T(1,128)S(1)}, f32[1,1280]{1,0:T(1,128)}, u32[]{:S(2)}) copy-start(f32[1,1280]{1,0:T(1,128)} %param.21) | copy-start | bytes 15364
  45.2 1.7 copy-start.3
  46.9 9.8 %collective-permute-start.7 = (bf16[3,4096]{1,0:T(4,128)(2,1)S(1)}, bf16[3,4096]{1,0:T(4,128)(2,1)S(1)}, u32[]{:S(2)}, u32[]{:S(2)}) collective-permute-start(bf16[3,4096]{1,0:T(4,128)(2,1)S(1)} %slice.201), channel_id=1, source_target_pairs={{0,8},{8,16},{16,24},{24,32},{32,40},{40,48},{48,56},{56,64},{64,7... | collective-permute-start | bytes 73736 | tf_op jit(solution)/shard_map/ppermute | solution.py:17
  180.5 1.3 copy-start
  180.5 2.9 copy-start.4
  181.9 3.9 copy-start.2
  181.9 1.5 copy-start.10
  192.7 65.4 %copy-start.12 = (u32[256]{0:T(256)S(1)}, u32[256]{0:T(256)}, u32[]{:S(2)}) copy-start(u32[256]{0:T(256)} %constant.128) | copy-start | bytes 3076
  258.0 66.4 %all-gather.8.cloned.1.call-start = ((), (), s32[]{:S(2)}) async-start(), calls=%async_computation.2 | async-start | bytes 1310720 | tf_op jit(solution)/shard_map/all_gather | solution.py:41
  300.2 80.7 %reduce-scatter.2.cloned.1.call-start = ((), (), s32[]{:S(2)}) async-start(), calls=%async_computation.3 | async-start | bytes 3538944 | tf_op jit(solution)/shard_map/reduce_scatter | solution.py:178
  308.8 15.7 %copy-start.11 = (f32[16]{0:T(128)S(1)}, f32[16]{0:T(128)}, u32[]{:S(2)}) copy-start(f32[16]{0:T(128)} %param.19) | copy-start | bytes 196
  329.2 2.0 copy-start.1
  329.2 2.7 copy-start.9
Sparse Core Ops, SparseCore 0:
  9.9 157.1 all-gather.5
  258.2 39.1 all-gather.9
  300.3 24.1 all-gather.7
  340.8 39.9 reduce-scatter.1
